TPU v7x, 32 devices: a whole 2x2x4 slice. The times are simulated.
32 devices in a mesh: samp: 16 (over z, y, x), tgt: 2 (over core).
Axes of the slice: x: 2, y: 2, z: 4, core: 2. Of those that a mesh axis runs over, the one named last changes fastest.
Arguments:
- samples: bfloat16 [3072, 128], P('samp'), may hold values from -6 to 6
- omega: bfloat16 [128, 4096], replicated, may hold values from -0.5 to 0.5
- phase: float32 [4096], replicated, may hold values from -3.140625 to 3.140625
- right_side: float32 [4096, 512], P('samp', 'tgt'), may hold values from -6 to 6
Outputs:
- weights: float32 [4096, 512], P('samp', 'tgt')
All inputs are finite; a program needn't handle non-finite values.
Results may differ from a plain program's by a relative error of at most 0.011.
The roundings to bfloat16 on the way count: a program that leaves them out, or rounds other values in their place, can miss the bound.
Values may be sent and summed in bfloat16 or wider, within the bound.
A program may use at most 128 MiB of HBM per device.

v0:
```python
import math
import jax
import jax.numpy as jnp
from jax import lax
from jax.sharding import PartitionSpec as P

ITERS = 2
ridge = 1.0


def precise_dot(left_matrix, right_matrix):
    return jnp.dot(left_matrix, right_matrix, precision=lax.Precision.HIGHEST)


def spd_solve(gram_matrix, rhs_matrix):
    factor = jnp.linalg.cholesky(gram_matrix)
    return jax.scipy.linalg.cho_solve((factor, True), rhs_matrix)


def cosine_block(samples, omega, phase, first_row, row_count):
    omega_cols = lax.dynamic_slice_in_dim(omega, first_row, row_count, 1)
    phase_cols = lax.dynamic_slice_in_dim(phase, first_row, row_count, 0)
    preact = jnp.dot(samples, omega_cols, preferred_element_type=jnp.float32) + phase_cols
    return jnp.cos(preact).astype(jnp.bfloat16)


def full_gram(stacked):
    summed = lax.psum(stacked, "samp")
    return lax.all_gather(summed, "tgt", axis=2, tiled=True)


def body(samples, omega, phase, right_side):
    feat_rows, col_count = right_side.shape
    samp_count = lax.axis_size("samp")
    feat_total = omega.shape[1]
    sample_total = samples.shape[0] * samp_count
    col_offset = lax.axis_index("tgt") * col_count
    store_block = math.gcd(feat_total, 512)
    stored = jnp.concatenate(
        [
            cosine_block(samples, omega, phase, index_block * store_block, store_block)
            for index_block in range(feat_total // store_block)
        ],
        axis=1,
    )

    def columns(first_row, row_count):
        return lax.dynamic_slice_in_dim(stored, first_row, row_count, 1)

    resid_all = lax.all_gather(right_side, "tgt", axis=1, tiled=True)
    direction_all = resid_all
    weight_own = jnp.zeros_like(right_side)
    gram_rr = full_gram(precise_dot(resid_all.T, right_side)[None])[0]
    for iteration in range(ITERS):
        direction_own = lax.dynamic_slice_in_dim(direction_all, col_offset, col_count, 1)
        initial = jnp.zeros((samples.shape[0], col_count), jnp.float32)
        shard_piece = lax.all_gather(direction_own.astype(jnp.bfloat16), "samp", axis=0, tiled=True)
        piece_rows = shard_piece.shape[0]
        block_size = math.gcd(piece_rows, 512)

        def project_one_block(index_block, acc_value):
            begin_row = index_block * block_size
            sub_piece = lax.dynamic_slice_in_dim(shard_piece, begin_row, block_size, 0)
            return acc_value + jnp.dot(
                columns(begin_row, block_size), sub_piece, preferred_element_type=jnp.float32
            )

        projected = lax.fori_loop(0, piece_rows // block_size, project_one_block, initial)
        proj_bf = projected.astype(jnp.bfloat16)
        transpose_row_count = feat_rows * lax.axis_size("samp")
        transpose_block_size = math.gcd(transpose_row_count, 512)

        def transpose_one_block(index_block, result):
            begin_row = index_block * transpose_block_size
            feats_block = columns(begin_row, transpose_block_size)
            block_term = lax.dot_general(
                feats_block, proj_bf, (((0,), (0,)), ((), ())), preferred_element_type=jnp.float32
            )
            return lax.dynamic_update_slice_in_dim(result, block_term, begin_row, 0)

        zero_rows = jnp.zeros((transpose_row_count, col_count), jnp.float32)
        summed_image = lax.psum_scatter(
            lax.fori_loop(
                0, transpose_row_count // transpose_block_size, transpose_one_block, zero_rows
            ),
            "samp",
            scatter_dimension=0,
            tiled=True,
        )
        image_own = summed_image / sample_total + ridge * direction_own
        image_all = lax.all_gather(image_own, "tgt", axis=1, tiled=True)
        gram_pq = full_gram(precise_dot(direction_all.T, image_own)[None])[0]
        alpha_coef = spd_solve(gram_pq, gram_rr)
        alpha_own = lax.dynamic_slice_in_dim(alpha_coef, col_offset, col_count, 1)
        weight_own = weight_own + precise_dot(direction_all, alpha_own)
        if iteration + 1 < ITERS:
            resid_all = resid_all - precise_dot(image_all, alpha_coef)
            resid_now = lax.dynamic_slice_in_dim(resid_all, col_offset, col_count, 1)
            gram_new = full_gram(precise_dot(resid_all.T, resid_now)[None])[0]
            beta_coef = spd_solve(gram_rr, gram_new)
            direction_all = resid_all + precise_dot(direction_all, beta_coef)
            gram_rr = gram_new
    return weight_own


def solution(mesh):
    placed = (P("samp", None), P(), P(), P("samp", "tgt"))
    return jax.shard_map(
        body, mesh=mesh, in_specs=placed, out_specs=P("samp", "tgt"), check_vma=False
    )
```

profile of v0, /device:TPU:0, one launch (start us, length us, event | category | flops | bytes accessed | tf_op | source)
XLA Modules:
  0.0 1215.1 jit_solution(10789328759363507932)
XLA Ops:
  22.8 50.4 %all-gather.7.cloned.1.call-done = bf16[4096,256]{1,0:T(8,128)(2,1)} async-done(((bf16[256,256]{1,0:T(8,128)(2,1)}), bf16[4096,256]{1,0:T(8,128)(2,1)}) %all-gather.7.cloned.1.call-update) | async-done | bytes 2097168 | tf_op jit(solution)/shard_map/all_gather | solution.py:57
  96.3 91.8 %reduce-scatter.3.cloned.1.call-done = f32[256,256]{1,0:T(8,128)} async-done(((f32[4096,256]{1,0:T(8,128)}), f32[256,256]{1,0:T(8,128)}) %reduce-scatter.3.cloned.1.call-update) | async-done | bytes 262160 | tf_op jit(solution)/shard_map/reduce_scatter | solution.py:82
  190.6 114.9 %all-reduce.10.cloned.1.call-done = (f32[1,512,256]{1,2,0:T(8,128)}, f32[1,512,256]{1,2,0:T(8,128)}) async-done(((f32[1,512,256]{1,2,0:T(8,128)}, f32[1,512,256]{1,2,0:T(8,128)}), (f32[1,512,256]{1,2,0:T(8,128)}, f32[1,512,256]{1,2,0:T(8,128)})) %all-reduce.10.cloned.1.call-update) | async-done | bytes 1048592 | tf_op jit(solution)/shard_map/psum | solution.py:28
  320.1 11.7 cholesky.374
  332.0 9.8 custom-call.35
  344.3 11.7 cholesky.393
  356.1 10.0 custom-call.36
  367.6 11.7 cholesky.414
  391.3 11.7 cholesky.431
  408.6 12.0 while.64
  420.6 39.3 %custom-call.38 = f32[4,128,128]{1,2,0:T(8,128)S(1)} custom-call(f32[4,128,128]{2,1,0:T(8,128)S(1)} %get-tuple-element.377), custom_call_target="InvertDiagBlocksLowerTriangular" | custom-call | tf_op jit(solution)/shard_map/jit(_cho_solve)/triangular_solve | solution.py:17
  475.0 11.7 cholesky.446
  487.5 10.8 custom-call.39
  502.1 12.5 %cholesky.465 = f32[128,128]{1,0:T(8,128)S(1)} custom-call(f32[128,128]{1,0:T(8,128)} %cholesky.603), custom_call_target="Cholesky" | custom-call | tf_op jit(solution)/shard_map/jit(cholesky)/cholesky | solution.py:16
  515.3 10.6 custom-call.40
  529.1 12.5 %cholesky.486 = f32[128,128]{1,0:T(8,128)} custom-call(f32[128,128]{1,0:T(8,128)S(1)} %cholesky.608), custom_call_target="Cholesky" | custom-call | tf_op jit(solution)/shard_map/jit(cholesky)/cholesky | solution.py:16
  543.1 10.4 custom-call.41
  555.9 12.3 %cholesky.503 = f32[128,128]{1,0:T(8,128)} custom-call(f32[128,128]{1,0:T(8,128)S(1)} %convolution_subtract_fusion.26), custom_call_target="Cholesky" | custom-call | tf_op jit(solution)/shard_map/jit(cholesky)/cholesky | solution.py:16
  578.3 105.3 %all-reduce.6.cloned.1.call-done = f32[1,512,256]{2,1,0:T(8,128)} async-done(((f32[1,512,256]{2,1,0:T(8,128)}), f32[1,512,256]{2,1,0:T(8,128)}) %all-reduce.6.cloned.1.call-update) | async-done | bytes 524304 | tf_op jit(solution)/shard_map/psum | solution.py:28
  684.4 14.8 %while.65 = (s32[]{:T(128)}, f32[512,512]{1,0:T(8,128)}, s32[4,2]{0,1:T(2,128)S(1)}, f32[4,128,128]{2,1,0:T(8,128)}, s32[]{:T(128)}) while((s32[]{:T(128)}, f32[512,512]{1,0:T(8,128)}, s32[4,2]{0,1:T(2,128)S(1)}, f32[4,128,128]{2,1,0:T(8,128)}, s32[]{:T(128)}) %tuple.227), condition=%wide.while_cond.clone, body=%wide.while_body.clone.sunk | while | flops 2 | bytes 132705 | solution.py:17
  699.2 40.8 %custom-call.42 = f32[4,128,128]{1,2,0:T(8,128)} custom-call(f32[4,128,128]{2,1,0:T(8,128)} %get-tuple-element.378), custom_call_target="InvertDiagBlocksLowerTriangular" | custom-call | tf_op jit(solution)/shard_map/jit(_cho_solve)/triangular_solve | solution.py:17
  752.9 59.5 %all-gather.15.cloned.1.call-done = bf16[4096,256]{1,0:T(8,128)(2,1)} async-done(((bf16[256,256]{1,0:T(8,128)(2,1)}), bf16[4096,256]{1,0:T(8,128)(2,1)}) %all-gather.15.cloned.1.call-update) | async-done | bytes 2097168 | tf_op jit(solution)/shard_map/all_gather | solution.py:57
  833.1 94.1 %reduce-scatter.5.cloned.1.call-done = f32[256,256]{1,0:T(8,128)} async-done(((f32[4096,256]{1,0:T(8,128)}), f32[256,256]{1,0:T(8,128)}) %reduce-scatter.5.cloned.1.call-update) | async-done | bytes 262160 | tf_op jit(solution)/shard_map/reduce_scatter | solution.py:82
  929.9 111.0 %all-reduce.8.cloned.1.call-done = f32[1,512,256]{1,2,0:T(8,128)} async-done(((f32[1,512,256]{1,2,0:T(8,128)}), f32[1,512,256]{1,2,0:T(8,128)}) %all-reduce.8.cloned.1.call-update) | async-done | bytes 524304 | tf_op jit(solution)/shard_map/psum | solution.py:28
  1055.6 11.7 cholesky.518
  1067.5 9.8 custom-call.43
  1079.8 11.7 cholesky.537
  1092.9 10.0 custom-call.44
  1104.4 11.7 cholesky.558
  1128.1 11.7 cholesky.575
  1144.4 11.5 while.66
  1155.9 39.3 %custom-call.46 = f32[4,128,128]{1,2,0:T(8,128)S(1)} custom-call(f32[4,128,128]{2,1,0:T(8,128)S(1)} %get-tuple-element.379), custom_call_target="InvertDiagBlocksLowerTriangular" | custom-call | tf_op jit(solution)/shard_map/jit(_cho_solve)/triangular_solve | solution.py:17
  (292 shorter events, 267.8 us)
Async XLA Ops:
  6.5 4.2 copy-start
  6.5 6.5 copy-start.26
  6.5 66.7 %all-gather.7.cloned.1.call-start = ((), (), s32[]{:S(2)}) async-start(), calls=%async_computation.2 | async-start | bytes 2228224 | tf_op jit(solution)/shard_map/all_gather | solution.py:57
  9.9 178.2 %reduce-scatter.3.cloned.1.call-start = ((), (), s32[]{:S(2)}) async-start(), calls=%async_computation.3 | async-start | bytes 4456448 | tf_op jit(solution)/shard_map/reduce_scatter | solution.py:82
  93.9 211.5 %all-reduce.10.cloned.1.call-start = ((), (), s32[]{:S(2)}) async-start(), calls=%async_computation.12 | async-start | bytes 2097152 | tf_op jit(solution)/shard_map/psum | solution.py:28
  190.5 124.4 %all-gather.9.cloned.1.call-start = ((), (), s32[]{:S(2)}) async-start(), calls=%async_computation.4 | async-start | bytes 1572864 | tf_op jit(solution)/shard_map/all_gather | solution.py:29
  305.5 154.5 %all-gather.11.cloned.1.call-start = ((), (), s32[]{:S(2)}) async-start(), calls=%async_computation.5 | async-start | bytes 1572864 | tf_op jit(solution)/shard_map/all_gather | solution.py:29
  307.8 375.8 %all-reduce.6.cloned.1.call-start = ((), (), s32[]{:S(2)}) async-start(), calls=%async_computation.6 | async-start | bytes 1048576 | tf_op jit(solution)/shard_map/psum | solution.py:28
  315.0 2.7 copy-start.9
  319.1 1.0 copy-start.15
  459.9 7.9 copy-start.20
  460.0 2.7 copy-start.1
  462.6 2.3 copy-start.7
  468.2 3.4 copy-start.21
  471.2 1.6 copy-start.2
  471.7 2.2 copy-start.10
  472.0 2.0 copy-start.12
  568.2 7.6 copy-start.25
  573.2 166.8 %all-gather.13.cloned.1.call-start = ((), (), s32[]{:S(2)}) async-start(), calls=%async_computation.7 | async-start | bytes 1572864 | tf_op jit(solution)/shard_map/all_gather | solution.py:29
  683.6 128.7 %all-gather.15.cloned.1.call-start = ((), (), s32[]{:S(2)}) async-start(), calls=%async_computation.8 | async-start | bytes 2228224 | tf_op jit(solution)/shard_map/all_gather | solution.py:57
  699.2 44.9 %copy-start.6 = (f32[512,512]{1,0:T(8,128)S(1)}, f32[512,512]{1,0:T(8,128)}, u32[]{:S(2)}) copy-start(f32[512,512]{1,0:T(8,128)} %get-tuple-element.842) | copy-start | bytes 3145732
  740.0 5.5 copy-start.22
  749.6 1.4 copy-start.5
  752.8 174.4 %reduce-scatter.5.cloned.1.call-start = ((), (), s32[]{:S(2)}) async-start(), calls=%async_computation.9 | async-start | bytes 4456448 | tf_op jit(solution)/shard_map/reduce_scatter | solution.py:82
  833.0 207.9 %copy-start.3 = (f32[128,512]{1,0:T(8,128)S(1)}, f32[128,512]{1,0:T(8,128)}, u32[]{:S(2)}) copy-start(f32[128,512]{1,0:T(8,128)} %copy-done.2) | copy-start | bytes 786436
  833.0 207.9 %copy-start.13 = (f32[128,512]{1,0:T(8,128)S(1)}, f32[128,512]{1,0:T(8,128)}, u32[]{:S(2)}) copy-start(f32[128,512]{1,0:T(8,128)} %copy-done.12) | copy-start | bytes 786436
  833.0 207.9 %copy-start.18 = (f32[128,512]{1,0:T(8,128)S(1)}, f32[128,512]{1,0:T(8,128)}, u32[]{:S(2)}) copy-start(f32[128,512]{1,0:T(8,128)} %fusion.170) | copy-start | bytes 786436
  833.0 207.9 %all-reduce.8.cloned.1.call-start = ((), (), s32[]{:S(2)}) async-start(), calls=%async_computation.10 | async-start | bytes 1048576 | tf_op jit(solution)/shard_map/psum | solution.py:28
  929.7 120.8 %all-gather.17.cloned.1.call-start = ((), (), s32[]{:S(2)}) async-start(), calls=%async_computation.11 | async-start | bytes 1572864 | tf_op jit(solution)/shard_map/all_gather | solution.py:29
  1050.5 2.7 copy-start.11
  1155.9 42.5 %copy-start.8 = (f32[512,512]{1,0:T(8,128)S(1)}, f32[512,512]{1,0:T(8,128)}, u32[]{:S(2)}) copy-start(f32[512,512]{1,0:T(8,128)} %get-tuple-element.844) | copy-start | bytes 3145732
  1204.9 1.4 copy-start.17
  (6 other events, 5.1 us)
Sparse Core Ops, SparseCore 0:
  10.1 63.1 all-gather.6
  94.0 94.0 reduce-scatter.2
  193.4 111.9 all-reduce.9
  306.8 8.0 all-gather.8
  316.4 10.1 all-gather.10
  573.3 110.2 all-reduce.5
  685.2 8.0 all-gather.12
  752.9 59.3 all-gather.14
  833.1 94.0 reduce-scatter.4
  932.2 108.6 all-reduce.7
  1042.4 8.0 all-gather.16
where the time goes:
time: 1230 us; the launch traced here: 1220 us
  waiting for transfers between devices  643 us (52%)
  other arithmetic  372 us (30%)
  matrix products  111 us (9%)
  local copies, waits for them, and re-layouts  60.6 us (5%)
  between operations  22.3 us (2%)
    psum x3, waiting for transfers between devices, full_gram(): summed = lax.psum(stacked, 'samp')  331 us
    another operation x43, other arithmetic, spd_solve(): factor = jnp.linalg.cholesky(gram_matrix)  243 us
    reduce_scatter x2, waiting for transfers between devices, body(): lax.psum_scatter(lax.fori_loop(0, transpose_row_count // transpose_block_...  186 us
    another operation x8, other arithmetic, spd_solve(): return jax.scipy.linalg.cho_solve((factor, True), rhs_matrix)  124 us
    all_gather x2, waiting for transfers between devices, body(): lax.all_gather(direction_own.astype(jnp.bfloat16), 'samp', axis=0, tiled=...  110 us
    another operation x40, local copies, waits for them, and re-layouts, spd_solve(): return jax.scipy.linalg.cho_solve((factor, True), rhs_matrix)  38.5 us
    another operation x42, matrix products, spd_solve(): return jax.scipy.linalg.cho_solve((factor, True), rhs_matrix)  31.8 us
  transfers between devices with their start and end apart: 11, of which 9 were waited for; matrix products, arithmetic and copies ran while one was open for 18% of the time, Pallas kernels for 0%

commit v1 on v0

--- a/solution.py
+++ b/solution.py
@@ -6,6 +6,28 @@
 
 ITERS = 2
 ridge = 1.0
+
+
+def joined_along(blocks, dim):
+    shape = list(blocks.shape[1:])
+    shape[dim] *= blocks.shape[0]
+    return jnp.moveaxis(blocks, 0, dim).reshape(shape)
+
+
+def collect(shard, axis, dim):
+    peers = lax.axis_size(axis)
+    pairs = [(i, (i + 1) % peers) for i in range(peers)]
+    back = [(b, a) for a, b in pairs]
+    lower, upper = ([], [])
+    for hop in range(peers - 1):
+        if hop % 2 == 0:
+            lower.append(lax.ppermute(lower[-1] if lower else shard, axis, pairs))
+        else:
+            upper.append(lax.ppermute(upper[-1] if upper else shard, axis, back))
+    blocks = jnp.stack([*lower[::-1], shard, *upper])
+    shift = lax.axis_index(axis) - len(lower)
+    blocks = blocks[(jnp.arange(peers) - shift) % peers]
+    return joined_along(blocks, dim)
 
 
 def precise_dot(left_matrix, right_matrix):
@@ -54,7 +76,7 @@
     for iteration in range(ITERS):
         direction_own = lax.dynamic_slice_in_dim(direction_all, col_offset, col_count, 1)
         initial = jnp.zeros((samples.shape[0], col_count), jnp.float32)
-        shard_piece = lax.all_gather(direction_own.astype(jnp.bfloat16), "samp", axis=0, tiled=True)
+        shard_piece = collect(direction_own.astype(jnp.bfloat16), "samp", 0)
         piece_rows = shard_piece.shape[0]
         block_size = math.gcd(piece_rows, 512)
 

time: 1230 us -> 1290 us (1.049)
  starting transfers between devices: 0.93 us -> 85.8 us
  waiting for transfers between devices: 643 us -> 567 us
  local copies, waits for them, and re-layouts: 60.6 us -> 99.8 us
    all_gather x2 -> x0, waiting for transfers between devices: 110 us -> none  [body(): lax.all_gather(direction_own.astype(jnp.bfloat16), 'samp', axis=0, tiled=...]
    ppermute x0 -> x30, starting transfers between devices: none -> 85.3 us  [the longest x14 80.5 us: collect(): upper.append(lax.ppermute(upper[-1] if upper else shard, axis, back))]
    ppermute x0 -> x30, waiting for transfers between devices: none -> 39.6 us  [the longest x16 36.5 us: collect(): lower.append(lax.ppermute(lower[-1] if lower else shard, axis, pairs))]
    unnamed x54 -> x108, local copies, waits for them, and re-layouts: 5.72 us -> 38.1 us
  transfers between devices with their start and end apart: 11 -> 39, of which waited for: 9 -> 26; matrix products, arithmetic and copies ran while one was open for 18% -> 20% of each run, Pallas kernels for 0% -> 0%
where the time goes in v1:
time: 1290 us; the launch traced here: 1280 us
  waiting for transfers between devices  567 us (44%)
  other arithmetic  380 us (29%)
  matrix products  117 us (9%)
  local copies, waits for them, and re-layouts  99.8 us (8%)
  starting transfers between devices  85.8 us (7%)
  between operations  22.4 us (2%)
    psum x3, waiting for transfers between devices, full_gram(): summed = lax.psum(stacked, 'samp')  331 us
    another operation x43, other arithmetic, spd_solve(): factor = jnp.linalg.cholesky(gram_matrix)  252 us
    reduce_scatter x2, waiting for transfers between devices, body(): lax.psum_scatter(lax.fori_loop(0, transpose_row_count // transpose_block_...  180 us
    another operation x8, other arithmetic, spd_solve(): return jax.scipy.linalg.cho_solve((factor, True), rhs_matrix)  124 us
    ppermute x14, starting transfers between devices, collect(): upper.append(lax.ppermute(upper[-1] if upper else shard, axis, back))  80.5 us
    unnamed x108, local copies, waits for them, and re-layouts  38.1 us
    another operation x40, local copies, waits for them, and re-layouts, spd_solve(): return jax.scipy.linalg.cho_solve((factor, True), rhs_matrix)  38 us
    ppermute x16, waiting for transfers between devices, collect(): lower.append(lax.ppermute(lower[-1] if lower else shard, axis, pairs))  36.5 us
  transfers between devices with their start and end apart: 39, of which 26 were waited for; matrix products, arithmetic and copies ran while one was open for 20% of the time, Pallas kernels for 0%

profile of v1, /device:TPU:0, one launch (start us, length us, event | category | flops | bytes accessed | tf_op | source)
XLA Modules:
  0.0 1278.3 jit_solution(14177337651745592348)
XLA Ops:
  124.4 88.9 %reduce-scatter.3.cloned.1.call-done = f32[256,256]{1,0:T(8,128)} async-done(((f32[4096,256]{1,0:T(8,128)}), f32[256,256]{1,0:T(8,128)}) %reduce-scatter.3.cloned.1.call-update) | async-done | bytes 262160 | tf_op jit(solution)/shard_map/reduce_scatter | solution.py:104
  215.8 114.8 %all-reduce.10.cloned.1.call-done = (f32[1,512,256]{1,2,0:T(8,128)}, f32[1,512,256]{1,2,0:T(8,128)}) async-done(((f32[1,512,256]{1,2,0:T(8,128)}, f32[1,512,256]{1,2,0:T(8,128)}), (f32[1,512,256]{1,2,0:T(8,128)}, f32[1,512,256]{1,2,0:T(8,128)})) %all-reduce.10.cloned.1.call-update) | async-done | bytes 1048592 | tf_op jit(solution)/shard_map/psum | solution.py:50
  345.4 11.7 cholesky.374
  357.2 9.8 custom-call.35
  369.6 11.7 cholesky.393
  381.3 18.5 %custom-call.36 = f32[1,128,128]{1,2,0:T(8,128)S(1)} custom-call(f32[1,128,128]{2,1,0:T(8,128)S(1)} %get-tuple-element.470), custom_call_target="InvertDiagBlocksLowerTriangular" | custom-call | tf_op jit(solution)/shard_map/jit(cholesky)/cholesky | solution.py:38
  401.4 11.7 cholesky.414
  413.8 9.8 custom-call.37
  425.1 11.7 cholesky.431
  442.3 11.5 while.64
  453.7 39.3 %custom-call.38 = f32[4,128,128]{1,2,0:T(8,128)S(1)} custom-call(f32[4,128,128]{2,1,0:T(8,128)S(1)} %get-tuple-element.377), custom_call_target="InvertDiagBlocksLowerTriangular" | custom-call | tf_op jit(solution)/shard_map/jit(_cho_solve)/triangular_solve | solution.py:39
  508.2 11.7 cholesky.446
  520.7 10.8 custom-call.39
  535.3 12.5 cholesky.465
  548.5 10.6 custom-call.40
  562.3 12.5 cholesky.486
  576.3 10.4 custom-call.41
  589.0 12.3 cholesky.503
  611.4 105.4 %all-reduce.6.cloned.1.call-done = f32[1,512,256]{2,1,0:T(8,128)} async-done(((f32[1,512,256]{2,1,0:T(8,128)}), f32[1,512,256]{2,1,0:T(8,128)}) %all-reduce.6.cloned.1.call-update) | async-done | bytes 524304 | tf_op jit(solution)/shard_map/psum | solution.py:50
  717.6 14.3 %while.65 = (s32[]{:T(128)}, f32[512,512]{1,0:T(8,128)}, s32[4,2]{0,1:T(2,128)S(1)}, f32[4,128,128]{2,1,0:T(8,128)}, s32[]{:T(128)}) while((s32[]{:T(128)}, f32[512,512]{1,0:T(8,128)}, s32[4,2]{0,1:T(2,128)S(1)}, f32[4,128,128]{2,1,0:T(8,128)}, s32[]{:T(128)}) %tuple.225), condition=%wide.while_cond.clone, body=%wide.while_body.clone.sunk | while | flops 2 | bytes 132705 | solution.py:39
  731.9 40.8 %custom-call.42 = f32[4,128,128]{1,2,0:T(8,128)} custom-call(f32[4,128,128]{2,1,0:T(8,128)} %get-tuple-element.378), custom_call_target="InvertDiagBlocksLowerTriangular" | custom-call | tf_op jit(solution)/shard_map/jit(_cho_solve)/triangular_solve | solution.py:39
  898.5 91.2 %reduce-scatter.5.cloned.1.call-done = f32[256,256]{1,0:T(8,128)} async-done(((f32[4096,256]{1,0:T(8,128)}), f32[256,256]{1,0:T(8,128)}) %reduce-scatter.5.cloned.1.call-update) | async-done | bytes 262160 | tf_op jit(solution)/shard_map/reduce_scatter | solution.py:104
  992.4 111.1 %all-reduce.8.cloned.1.call-done = f32[1,512,256]{1,2,0:T(8,128)} async-done(((f32[1,512,256]{1,2,0:T(8,128)}), f32[1,512,256]{1,2,0:T(8,128)}) %all-reduce.8.cloned.1.call-update) | async-done | bytes 524304 | tf_op jit(solution)/shard_map/psum | solution.py:50
  1118.2 11.7 cholesky.518
  1130.1 9.8 custom-call.43
  1142.4 11.7 cholesky.537
  1155.5 10.0 custom-call.44
  1167.1 11.7 cholesky.558
  1179.5 9.8 custom-call.45
  1190.7 11.7 cholesky.575
  1207.0 12.0 while.66
  1219.0 39.3 %custom-call.46 = f32[4,128,128]{1,2,0:T(8,128)S(1)} custom-call(f32[4,128,128]{2,1,0:T(8,128)S(1)} %get-tuple-element.379), custom_call_target="InvertDiagBlocksLowerTriangular" | custom-call | tf_op jit(solution)/shard_map/jit(_cho_solve)/triangular_solve | solution.py:39
  (406 shorter events, 418.4 us)
Async XLA Ops:
  6.5 206.8 %reduce-scatter.3.cloned.1.call-start = ((), (), s32[]{:S(2)}) async-start(), calls=%async_computation.2 | async-start | bytes 4456448 | tf_op jit(solution)/shard_map/reduce_scatter | solution.py:104
  9.2 12.4 collective-permute-start
  12.1 20.7 %collective-permute-start.8 = (bf16[256,256]{1,0:T(8,128)(2,1)S(1)}, bf16[256,256]{1,0:T(8,128)(2,1)S(1)}, u32[]{:S(2)}, u32[]{:S(2)}) collective-permute-start(bf16[256,256]{1,0:T(8,128)(2,1)S(1)} %dynamic-slice_convert_fusion.1), channel_id=1, source_target_pairs={{2,0},{4,2},{6,4},{8,6},{10,8},{12,10},{14,12},{16,14},{18,16},{20... | collective-permute-start | bytes 393224 | tf_op jit(solution)/shard_map/ppermute | solution.py:26
  21.6 8.9 collective-permute-start.1
  30.5 8.7 collective-permute-start.2
  32.8 8.7 collective-permute-start.9
  47.7 8.6 collective-permute-start.4
  50.0 8.7 collective-permute-start.11
  58.7 8.8 collective-permute-start.12
  64.9 8.9 collective-permute-start.6
  73.8 8.9 collective-permute-start.7
  75.8 21.2 %collective-permute-start.14 = (bf16[256,256]{1,0:T(8,128)(2,1)}, bf16[256,256]{1,0:T(8,128)(2,1)S(1)}, u32[]{:S(2)}, u32[]{:S(2)}) collective-permute-start(bf16[256,256]{1,0:T(8,128)(2,1)} %collective-permute-done.13), channel_id=1, source_target_pairs={{2,0},{4,2},{6,4},{8,6},{10,8},{12,10},{14,12},{16,14},{18,16},{20... | collective-permute-start | bytes 393224 | tf_op jit(solution)/shard_map/ppermute | solution.py:26
  122.0 208.6 %all-reduce.10.cloned.1.call-start = ((), (), s32[]{:S(2)}) async-start(), calls=%async_computation.10 | async-start | bytes 2097152 | tf_op jit(solution)/shard_map/psum | solution.py:50
  215.7 124.6 %all-gather.5.cloned.1.call-start = ((), (), s32[]{:S(2)}) async-start(), calls=%async_computation.3 | async-start | bytes 1572864 | tf_op jit(solution)/shard_map/all_gather | solution.py:51
  330.6 162.5 %all-gather.7.cloned.1.call-start = ((), (), s32[]{:S(2)}) async-start(), calls=%async_computation.4 | async-start | bytes 1572864 | tf_op jit(solution)/shard_map/all_gather | solution.py:51
  333.0 383.8 %all-reduce.6.cloned.1.call-start = ((), (), s32[]{:S(2)}) async-start(), calls=%async_computation.5 | async-start | bytes 1048576 | tf_op jit(solution)/shard_map/psum | solution.py:50
  606.4 166.4 %all-gather.9.cloned.1.call-start = ((), (), s32[]{:S(2)}) async-start(), calls=%async_computation.6 | async-start | bytes 1572864 | tf_op jit(solution)/shard_map/all_gather | solution.py:51
  716.8 272.9 %reduce-scatter.5.cloned.1.call-start = ((), (), s32[]{:S(2)}) async-start(), calls=%async_computation.7 | async-start | bytes 4456448 | tf_op jit(solution)/shard_map/reduce_scatter | solution.py:104
  784.9 8.7 collective-permute-start.15
  793.6 8.6 collective-permute-start.23
  810.7 9.0 collective-permute-start.18
  810.7 9.1 collective-permute-start.25
  819.7 10.0 collective-permute-start.19
  819.8 9.9 collective-permute-start.26
  829.7 9.0 collective-permute-start.20
  830.4 8.7 collective-permute-start.27
  838.7 8.8 collective-permute-start.21
  839.1 9.1 collective-permute-start.28
  847.5 8.9 collective-permute-start.22
  848.2 25.2 %collective-permute-start.29 = (bf16[256,256]{1,0:T(8,128)(2,1)}, bf16[256,256]{1,0:T(8,128)(2,1)S(1)}, u32[]{:S(2)}, u32[]{:S(2)}) collective-permute-start(bf16[256,256]{1,0:T(8,128)(2,1)} %collective-permute-done.28), channel_id=1, source_target_pairs={{2,0},{4,2},{6,4},{8,6},{10,8},{12,10},{14,12},{16,14},{18,16},{20... | collective-permute-start | bytes 393224 | tf_op jit(solution)/shard_map/ppermute | solution.py:26
  898.5 205.0 %all-reduce.8.cloned.1.call-start = ((), (), s32[]{:S(2)}) async-start(), calls=%async_computation.8 | async-start | bytes 1048576 | tf_op jit(solution)/shard_map/psum | solution.py:50
  992.2 120.9 %all-gather.11.cloned.1.call-start = ((), (), s32[]{:S(2)}) async-start(), calls=%async_computation.9 | async-start | bytes 1572864 | tf_op jit(solution)/shard_map/all_gather | solution.py:51
  (46 other events, 1008.3 us)
Sparse Core Ops, SparseCore 0:
  122.2 91.0 reduce-scatter.2
  218.6 111.9 all-reduce.9
  332.1 8.0 all-gather.4
  341.7 10.2 all-gather.6
  606.5 110.2 all-reduce.5
  718.2 8.0 all-gather.8
  898.6 91.0 reduce-scatter.4
  994.9 108.5 all-reduce.7
  1105.1 8.0 all-gather.10
